TPU v7x, 32 devices: a whole 2x2x4 slice. The times are simulated.
32 devices in a mesh: row: 8 (over z, x), col: 4 (over y, core).
Axes of the slice: x: 2, y: 2, z: 4, core: 2. Of those that a mesh axis runs over, the one named last changes fastest.
Arguments:
- t2_amps: bfloat16 [16384, 49152], P('row', 'col'), may hold values from -0.5 to 0.5
- l2_amps: bfloat16 [256, 49152], P('row', 'col'), may hold values from -0.02734375 to 0.02734375
Outputs:
- ladder: bfloat16 [256, 49152], P('row', 'col')
All inputs are finite; a program needn't handle non-finite values.
Results may differ from a plain program's by a relative error of at most 0.0044.
Values may be sent and summed in bfloat16 or wider, within the bound.
A program may use at most 128 MiB of HBM per device.

v0:
```python
import jax
import jax.numpy as jnp
from jax import lax
from jax.sharding import PartitionSpec as P


def on_device(t2_amps, l2_amps):
    partial_value = jnp.dot(
        t2_amps,
        lax.all_gather(l2_amps, "row", axis=0, tiled=True).T,
        preferred_element_type=jnp.float32,
    )
    oooo = lax.psum(partial_value, "col")
    oooo_half = oooo.astype(jnp.bfloat16)
    ladder = lax.psum_scatter(
        lax.dot_general(
            oooo_half, t2_amps, (((0,), (0,)), ((), ())), preferred_element_type=jnp.float32
        ),
        "row",
        scatter_dimension=0,
        tiled=True,
    )
    return ladder.astype(jnp.bfloat16)


def solution(mesh):
    return jax.shard_map(
        on_device,
        mesh=mesh,
        in_specs=(P("row", "col"), P("row", "col")),
        out_specs=P("row", "col"),
        check_vma=False,
    )
```

profile of v0, /device:TPU:0, one launch (start us, length us, event | category | flops | bytes accessed | tf_op | source)
XLA Modules:
  0.0 413.1 jit_solution(6841744538810563476)
XLA Ops:
  6.5 0.0 all-gather.2.cloned.1.call-start
  6.5 0.7 all-gather.2.cloned.1.call-update
  7.3 0.0 reduce-scatter.2.cloned.1.call-start
  7.3 103.7 %all-gather.2.cloned.1.call-done = bf16[256,12288]{1,0:T(8,128)(2,1)} async-done(((bf16[32,12288]{1,0:T(8,128)(2,1)}), bf16[256,12288]{1,0:T(8,128)(2,1)}) %all-gather.2.cloned.1.call-update) | async-done | bytes 6291472 | tf_op jit(solution)/shard_map/all_gather | solution.py:10
  111.0 21.7 %fusion.2 = f32[2048,256]{1,0:T(8,128)S(1)} fusion(bf16[2048,12288]{1,0:T(8,128)(2,1)} %param.2, bf16[256,12288]{1,0:T(8,128)(2,1)} %all-gather.2.cloned.1.call-done), kind=kOutput, calls=%fused_computation.2 | convolution fusion | flops 12884901888 | bytes 58720256 | tf_op jit(solution)/shard_map/dot_general | solution.py:8
  132.6 40.2 %all-reduce.1 = bf16[2048,256]{1,0:T(8,128)(2,1)S(1)} all-reduce(f32[2048,256]{1,0:T(8,128)S(1)} %fusion.2), channel_id=1, replica_groups=mesh['row'=8,'col'=4] {'col'}, use_global_device_ids=true, to_apply=%region_0.0 | all-reduce | flops 524288 | bytes 3145728 | tf_op jit(solution)/shard_map/psum | solution.py:13
  172.8 24.8 %fusion.3 = f32[256,12288]{1,0:T(8,128)} fusion(bf16[2048,256]{1,0:T(8,128)(2,1)S(1)} %all-reduce.1, bf16[2048,12288]{1,0:T(8,128)(2,1)} %param.2), kind=kOutput, calls=%fused_computation.3 | convolution fusion | flops 12884901888 | bytes 63963136 | tf_op jit(solution)/shard_map/dot_general | solution.py:16
  197.6 0.0 reduce-scatter.2.cloned.1.call-update
  197.6 206.2 %reduce-scatter.2.cloned.1.call-done = f32[32,12288]{1,0:T(8,128)} async-done(((f32[256,12288]{1,0:T(8,128)}), f32[32,12288]{1,0:T(8,128)}) %reduce-scatter.2.cloned.1.call-update) | async-done | bytes 1572880 | tf_op jit(solution)/shard_map/reduce_scatter | solution.py:15
  403.9 2.4 convert_element_type.7
Async XLA Ops:
  6.5 104.4 %all-gather.2.cloned.1.call-start = ((), (), s32[]{:S(2)}) async-start(), calls=%async_computation.1 | async-start | bytes 7077888 | tf_op jit(solution)/shard_map/all_gather | solution.py:10
  7.3 396.6 %reduce-scatter.2.cloned.1.call-start = ((), (), s32[]{:S(2)}) async-start(), calls=%async_computation.2 | async-start | bytes 14155776 | tf_op jit(solution)/shard_map/reduce_scatter | solution.py:15
Sparse Core Ops, SparseCore 0:
  9.5 101.4 all-gather.1
  197.7 206.0 reduce-scatter.1
where the time goes:
time: 413 us
  waiting for transfers between devices  311 us (75%)
  matrix products  46.4 us (11%)
  blocking collectives  40.2 us (10%)
  between operations  13.4 us (3%)
    reduce_scatter x1, waiting for transfers between devices, on_device(): lax.psum_scatter(lax.dot_general(oooo_half, t2_amps, (((0,), (0,)), ((),...  206 us
    all_gather x1, waiting for transfers between devices, on_device(): lax.all_gather(l2_amps, 'row', axis=0, tiled=True)  104 us
    psum x1, blocking collectives, on_device(): oooo = lax.psum(partial_value, 'col')  40.2 us
    dot_general x1, matrix products, on_device(): lax.dot_general(oooo_half, t2_amps, (((0,), (0,)), ((), ())), preferred_e...  24.8 us
    dot_general x1, matrix products, on_device(): jnp.dot(t2_amps, lax.all_gather(l2_amps, 'row', axis=0, tiled=True).T, pr...  21.7 us
  transfers between devices with their start and end apart: 2, of which 2 were waited for; matrix products, arithmetic and copies ran while one was open for 0% of the time, Pallas kernels for 0%

commit v1 on v0

v1 whole, which is shorter than its diff:
```python
import functools

import jax
import jax.numpy as jnp
from jax import lax
from jax.experimental import pallas as pl
from jax.experimental.pallas import tpu as pltpu
from jax.sharding import PartitionSpec as P

MESH = pl.DeviceIdType.MESH
HALVES = 2
SLABS = 3
STREAMS = 4
CHUNKS_1 = 8
CHUNKS_2 = 8
BUFFERS = 3


def row_of(position, rows):
    upper = lax.div(position, rows // 2)
    return 2 * position + upper * (2 * rows - 1 - 4 * position)


def kernel(R, C, t2, l2, out, gath, acc, res, recv_a, sum_b, recv_b, half, half_t,
           rs_send, rs_recv, buf1, buf2, ag_ss, ag_rs, r_ss, r_rs, sem1, sem2,
           own_sem, a_sem, b_sem, c_sem, d_sem):
    IJ, AB = t2.shape
    H, Q, U = HALVES, SLABS, STREAMS
    KR = l2.shape[0] // H
    W = AB // Q
    WM = W // U
    n_short = R // 2 - 1
    TS = U * (R - 1) // 2
    AGS = H * Q
    chips = C // 2
    hij = IJ // 2
    bij = hij // chips
    rows1 = IJ // CHUNKS_1
    cols2 = W // CHUNKS_2

    my_row = lax.axis_index("row")
    my_col = lax.axis_index("col")
    a0, b0 = lax.div(my_row, 2), lax.rem(my_row, 2)
    me = a0 + b0 * (R - 1 - 2 * a0)
    ring = [row_of(lax.rem(me + 1, R), R), row_of(lax.rem(me + R - 1, R), R)]
    core = lax.rem(my_col, 2)
    chip = lax.div(my_col, 2)
    sibling = my_col + 1 - 2 * core

    def peer(d):
        return 2 * lax.rem(chip + d, chips) + core

    def block_row(offset):
        return pl.multiple_of(row_of(lax.rem(me + offset + 2 * R, R), R) * KR, KR)

    def dma1(c):
        a, i = lax.div(c, CHUNKS_1), lax.rem(c, CHUNKS_1)
        slot = lax.rem(c, BUFFERS)
        return pltpu.make_async_copy(
            t2.at[pl.ds(pl.multiple_of(i * rows1, rows1), rows1),
                  pl.ds(pl.multiple_of(lax.rem(a, Q) * W, W), W)],
            buf1.at[slot], sem1.at[slot])

    def dma2(c):
        slot = lax.rem(c, BUFFERS)
        k = lax.rem(c, Q * CHUNKS_2)
        return pltpu.make_async_copy(
            t2.at[:, pl.ds(pl.multiple_of(k * cols2, cols2), cols2)],
            buf2.at[slot], sem2.at[slot])

    def own(g):
        return pltpu.make_async_copy(
            l2.at[pl.ds(g * KR, KR), :], gath.at[g, pl.ds(block_row(0), KR), :],
            own_sem.at[g])

    for g in range(H):
        own(g).start()

    barrier = pltpu.get_barrier_semaphore()
    for r in ring:
        pl.semaphore_signal(barrier, inc=1, device_id=(r, my_col), device_id_type=MESH)
    pl.semaphore_signal(barrier, inc=1, device_id=(my_row, sibling), device_id_type=MESH)
    for d in range(1, chips):
        pl.semaphore_signal(barrier, inc=1, device_id=(my_row, peer(d)), device_id_type=MESH)
    pl.semaphore_wait(barrier, 2 + chips)

    for c in range(BUFFERS):
        dma1(jnp.int32(c)).start()
    for g in range(H):
        own(g).wait()

    def split(t):
        h = lax.div(t, U)
        last = lax.div(h, n_short)
        v = lax.rem(t, U) * (1 + last)
        return h, v

    def stream(v, d):
        return v if d == 0 else v + 1 - 2 * lax.rem(v, 2)

    def hops(v):
        return n_short + 1 - lax.rem(v, 2)

    def last_tick(v):
        odd = lax.rem(v, 2)
        return odd * ((n_short - 1) * U + v) + (1 - odd) * (n_short * U + lax.div(v, 2))

    def ag_copy(a, t, d):
        g, q = lax.div(a, Q), lax.rem(a, Q)
        h, v = split(t)
        u = stream(v, d)
        off = -h if d == 0 else h
        view = gath.at[g, pl.ds(block_row(off), KR),
                       pl.ds(pl.multiple_of(q * W + u * WM, WM), WM)]
        return pltpu.make_async_remote_copy(
            src_ref=view, dst_ref=view, send_sem=ag_ss.at[d, a, t], recv_sem=ag_rs.at[d, a, t],
            device_id=(ring[d], my_col), device_id_type=MESH)

    def ag_recv(a, t, d):
        g, q = lax.div(a, Q), lax.rem(a, Q)
        h, v = split(t)
        u = stream(v, d)
        off = -(h + 1) if d == 0 else h + 1
        view = gath.at[g, pl.ds(block_row(off), KR),
                       pl.ds(pl.multiple_of(q * W + u * WM, WM), WM)]
        return pltpu.make_async_remote_copy(
            src_ref=view, dst_ref=view, send_sem=ag_ss.at[d, a, t], recv_sem=ag_rs.at[d, a, t],
            device_id=(ring[d], my_col), device_id_type=MESH)

    def rs_copy(b, t, d):
        return pltpu.make_async_remote_copy(
            src_ref=rs_send.at[d, b, t], dst_ref=rs_recv.at[d, b, t],
            send_sem=r_ss.at[d, b, t], recv_sem=r_rs.at[d, b, t],
            device_id=(ring[d], my_col), device_id_type=MESH)

    def ag_tick(a, t):
        h, v = split(t)
        for d in range(2):
            @pl.when(h > 0)
            def _():
                ag_recv(a, t - U + (v - lax.rem(t, U)), d).wait_recv()
            ag_copy(a, t, d).start()

            @pl.when(a > 0)
            def _():
                ag_copy(a - 1, t, d).wait_send()

    def ag_finish(a):
        def one(v, _):
            for d in range(2):
                ag_recv(a, last_tick(v), d).wait_recv()
            return 0
        lax.fori_loop(0, U, one, 0)

    def rs_part(b, offset, u):
        return res[lax.rem(b, 2), pl.ds(block_row(offset), KR),
                   pl.ds(pl.multiple_of(u * WM, WM), WM)]

    def rs_tick(b, t):
        h, v = split(t)
        for d in range(2):
            u = stream(v, d)
            off = hops(v) - h
            off = off if d == 0 else -off

            @pl.when(h == 0)
            def _():
                rs_send[d, b, t] = rs_part(b, off, u).astype(jnp.bfloat16)

            @pl.when(h > 0)
            def _():
                before = t - U + (v - lax.rem(t, U))
                rs_copy(b, before, d).wait_recv()
                rs_send[d, b, t] = (
                    rs_part(b, off, u) + rs_recv[d, b, before].astype(jnp.float32)
                ).astype(jnp.bfloat16)
            rs_copy(b, t, d).start()

            @pl.when(b > 0)
            def _():
                rs_copy(b - 1, t, d).wait_send()

    def rs_finish(b):
        g, q = lax.div(b, Q), lax.rem(b, Q)

        def one(u, _):
            w = u + 1 - 2 * lax.rem(u, 2)
            rs_copy(b, last_tick(u), 0).wait_recv()
            rs_copy(b, last_tick(w), 1).wait_recv()
            total = (rs_part(b, 0, u) + rs_recv[0, b, last_tick(u)].astype(jnp.float32)
                     + rs_recv[1, b, last_tick(w)].astype(jnp.float32))
            out[pl.ds(pl.multiple_of(g * KR, KR), KR),
                pl.ds(pl.multiple_of(q * W + u * WM, WM), WM)] = total.astype(jnp.bfloat16)
            return 0
        lax.fori_loop(0, U, one, 0)

    def phase1(a, i):
        c = a * CHUNKS_1 + i
        g, q = lax.div(a, Q), lax.rem(a, Q)
        dma1(c).wait()
        part = lax.dot_general(
            buf1[lax.rem(c, BUFFERS)],
            gath[g, :, pl.ds(pl.multiple_of(q * W, W), W)],
            (((1,), (1,)), ((), ())), preferred_element_type=jnp.float32)
        where = pl.ds(pl.multiple_of(i * rows1, rows1), rows1)

        @pl.when(q == 0)
        def _():
            acc[g, where, :] = part

        @pl.when(q > 0)
        def _():
            acc[g, where, :] += part

        @pl.when(c + BUFFERS < AGS * CHUNKS_1)
        def _():
            dma1(c + BUFFERS).start()

    def phase2(b, i):
        c = b * CHUNKS_2 + i
        dma2(c).wait()
        res[lax.rem(b, 2), :, pl.ds(pl.multiple_of(i * cols2, cols2), cols2)] = jnp.dot(
            half_t[lax.div(b, Q)], buf2[lax.rem(c, BUFFERS)],
            preferred_element_type=jnp.float32)

        @pl.when(c + BUFFERS < AGS * CHUNKS_2)
        def _():
            dma2(c + BUFFERS).start()

    mine = pl.multiple_of(core * hij, hij)
    other = pl.multiple_of((1 - core) * hij, hij)
    my_block = pl.multiple_of(chip * bij, bij)

    def copy_a(g):
        return pltpu.make_async_remote_copy(
            src_ref=acc.at[g, pl.ds(other, hij), :], dst_ref=recv_a.at[g],
            send_sem=a_sem.at[0, g], recv_sem=a_sem.at[1, g],
            device_id=(my_row, sibling), device_id_type=MESH)

    def copy_b(g, d):
        return pltpu.make_async_remote_copy(
            src_ref=sum_b.at[g, pl.ds(pl.multiple_of(lax.rem(chip + d, chips) * bij, bij), bij), :],
            dst_ref=recv_b.at[g, d - 1],
            send_sem=b_sem.at[0, g, d - 1], recv_sem=b_sem.at[1, g, d - 1],
            device_id=(my_row, peer(d)), device_id_type=MESH)

    def copy_c(g, d, sender):
        view = half.at[g, pl.ds(pl.multiple_of(mine + sender * bij, bij), bij), :]
        return pltpu.make_async_remote_copy(
            src_ref=view, dst_ref=view,
            send_sem=c_sem.at[0, g, d - 1], recv_sem=c_sem.at[1, g, d - 1],
            device_id=(my_row, peer(d)), device_id_type=MESH)

    def copy_d(g, where):
        view = half.at[g, pl.ds(where, hij), :]
        return pltpu.make_async_remote_copy(
            src_ref=view, dst_ref=view, send_sem=d_sem.at[0, g], recv_sem=d_sem.at[1, g],
            device_id=(my_row, sibling), device_id_type=MESH)

    def stage_a(g):
        copy_a(g).start()

    def stage_b(g):
        copy_a(g).wait_recv()
        sum_b[g] = acc[g, pl.ds(mine, hij), :] + recv_a[g]
        for d in range(1, chips):
            copy_b(g, d).start()

    def stage_c(g):
        total = sum_b[g, pl.ds(my_block, bij), :]
        for d in range(1, chips):
            copy_b(g, d).wait_recv()
            total = total + recv_b[g, d - 1]
        half[g, pl.ds(pl.multiple_of(mine + my_block, bij), bij), :] = total.astype(jnp.bfloat16)
        for d in range(1, chips):
            copy_c(g, d, chip).start()

    def stage_d(g):
        for d in range(1, chips):
            copy_c(g, d, lax.rem(chip + chips - d, chips)).wait_recv()
        copy_d(g, mine).start()

    def stage_e(g):
        copy_d(g, other).wait_recv()

        step = 256

        def turn(i, _):
            at = pl.multiple_of(i * step, step)
            half_t[g, :, pl.ds(at, step)] = (
                half[g, pl.ds(at, step), :].astype(jnp.float32).T.astype(jnp.bfloat16))
            return 0
        lax.fori_loop(0, IJ // step, turn, 0)
        copy_a(g).wait_send()
        copy_d(g, mine).wait_send()
        for d in range(1, chips):
            copy_b(g, d).wait_send()
            copy_c(g, d, chip).wait_send()

    first1 = U
    first2 = TS - CHUNKS_2
    begin = first1 + CHUNKS_1
    finish = (Q - 1) * TS + first2 - 1 if Q > 1 else TS
    room = finish - begin
    events = [
        (begin, stage_a),
        (begin + 1, stage_b),
        (begin + 1 + (room - 2) * 6 // 10, stage_c),
        (begin + 1 + (room - 2) * 6 // 10 + (room - 2) * 4 // 10, stage_d),
        (finish, stage_e),
    ]

    def body(T, _):
        s, t = lax.div(T, TS), lax.rem(T, TS)

        @pl.when(s < AGS)
        def _():
            ag_tick(s, t)

        @pl.when(s >= AGS)
        def _():
            rs_tick(s - AGS, t)

        @pl.when((t == U - 1) & (s > 0) & (s <= AGS))
        def _():
            ag_finish(s - 1)

        @pl.when((t == U - 1) & (s > AGS))
        def _():
            rs_finish(s - 1 - AGS)

        @pl.when(T == TS)
        def _():
            for c in range(BUFFERS):
                dma2(jnp.int32(c)).start()

        @pl.when((s > 0) & (s <= AGS) & (t >= first1) & (t < first1 + CHUNKS_1))
        def _():
            phase1(s - 1, t - first1)

        for when, stage in events:
            since = T - when
            g = lax.div(since, Q * TS) - 1
            @pl.when((since >= Q * TS) & (lax.rem(since, Q * TS) == 0) & (g < H))
            def _():
                stage(g)

        @pl.when((s >= AGS - 1) & (s < 2 * AGS - 1) & (t >= first2))
        def _():
            phase2(s - (AGS - 1), t - first2)
        return 0

    lax.fori_loop(0, 2 * AGS * TS, body, 0)
    rs_finish(jnp.int32(AGS - 1))

    def drain(t, _):
        for d in range(2):
            ag_copy(AGS - 1, t, d).wait_send()
            rs_copy(AGS - 1, t, d).wait_send()
        return 0
    lax.fori_loop(0, TS, drain, 0)


def on_device(R, C, t2_amps, l2_amps):
    IJ, AB = t2_amps.shape
    H, Q, U = HALVES, SLABS, STREAMS
    KR = l2_amps.shape[0] // H
    K = KR * R
    W = AB // Q
    WM = W // U
    TS = U * (R - 1) // 2
    S = H * Q
    chips = C // 2
    hij = IJ // 2
    dma = pltpu.SemaphoreType.DMA
    return pl.pallas_call(
        functools.partial(kernel, R, C),
        out_shape=jax.ShapeDtypeStruct(l2_amps.shape, jnp.bfloat16),
        in_specs=[pl.BlockSpec(memory_space=pl.ANY)] * 2,
        out_specs=pl.BlockSpec(memory_space=pltpu.VMEM),
        scratch_shapes=[
            pltpu.VMEM((H, K, AB), jnp.bfloat16),
            pltpu.VMEM((H, IJ, K), jnp.float32),
            pltpu.VMEM((2, K, W), jnp.float32),
            pltpu.VMEM((H, hij, K), jnp.float32),
            pltpu.VMEM((H, hij, K), jnp.float32),
            pltpu.VMEM((H, chips - 1, hij // chips, K), jnp.float32),
            pltpu.VMEM((H, IJ, K), jnp.bfloat16),
            pltpu.VMEM((H, K, IJ), jnp.bfloat16),
            pltpu.VMEM((2, S, TS, KR, WM), jnp.bfloat16),
            pltpu.VMEM((2, S, TS, KR, WM), jnp.bfloat16),
            pltpu.VMEM((BUFFERS, IJ // CHUNKS_1, W), jnp.bfloat16),
            pltpu.VMEM((BUFFERS, IJ, W // CHUNKS_2), jnp.bfloat16),
            dma((2, S, TS)), dma((2, S, TS)), dma((2, S, TS)), dma((2, S, TS)),
            dma((BUFFERS,)), dma((BUFFERS,)), dma((H,)),
            dma((2, H)), dma((2, H, chips - 1)), dma((2, H, chips - 1)), dma((2, H)),
        ],
        compiler_params=pltpu.CompilerParams(
            collective_id=0, has_side_effects=True, vmem_limit_bytes=67000000),
    )(t2_amps, l2_amps)


def solution(mesh):
    R, C = mesh.shape["row"], mesh.shape["col"]
    return jax.shard_map(
        functools.partial(on_device, R, C),
        mesh=mesh,
        in_specs=(P("row", "col"), P("row", "col")),
        out_specs=P("row", "col"),
        check_vma=False,
    )
```

time: 413 us -> 166 us (0.40)
  waiting for transfers between devices: 311 us -> 0 us
  Pallas kernels: 0 us -> 164 us
  matrix products: 46.4 us -> 0 us
  blocking collectives: 40.2 us -> 0 us
  between operations: 13.4 us -> 0.01 us
    reduce_scatter x1 -> x0, waiting for transfers between devices: 206 us -> none  [on_device(): lax.psum_scatter(lax.dot_general(oooo_half, t2_amps, (((0,), (0,)), ((),...]
    pallas_call x0 -> x1, Pallas kernels: none -> 164 us  [on_device(): pl.pallas_call(functools.partial(kernel, R, C), out_shape=jax.ShapeDtypeS...]
    all_gather x1 -> x0, waiting for transfers between devices: 104 us -> none  [on_device(): lax.all_gather(l2_amps, 'row', axis=0, tiled=True)]
    dot_general x2 -> x0, matrix products: 46.4 us -> none  [the longest x1 24.8 us: on_device(): lax.dot_general(oooo_half, t2_amps, (((0,), (0,)), ((), ())), preferred_e...]
    psum x1 -> x0, blocking collectives: 40.2 us -> none  [on_device(): oooo = lax.psum(partial_value, 'col')]
  transfers between devices with their start and end apart: 2 -> 0, of which waited for: 2 -> 0; matrix products, arithmetic and copies ran while one was open for 0% -> 0% of each run, Pallas kernels for 0% -> 0%
where the time goes in v1:
time: 166 us
  Pallas kernels  164 us (99%)
  local copies, waits for them, and re-layouts  2.06 us (1%)
    pallas_call x1, Pallas kernels, on_device(): pl.pallas_call(functools.partial(kernel, R, C), out_shape=jax.ShapeDtypeS...  164 us

profile of v1, /device:TPU:0, one launch (start us, length us, event | category | flops | bytes accessed | tf_op | source)
XLA Modules:
  0.0 165.6 jit_solution(2776353335472064695)
XLA Ops:
  0.0 163.5 %shard_map.28 = bf16[32,12288]{1,0:T(8,128)(2,1)} custom-call(bf16[2048,12288]{1,0:T(8,128)(2,1)} %t2.1, bf16[32,12288]{1,0:T(8,128)(2,1)} %l2.1), custom_call_target="tpu_custom_call" | custom-call | tf_op jit(solution)/shard_map/pallas_call | solution.py:376
  163.5 2.1 %copy.4 = bf16[32,12288]{1,0:T(8,128)(2,1)} copy(bf16[32,12288]{1,0:T(8,128)(2,1)} %shard_map.28) | data formatting | bytes 1572864

commit v2 on v1

--- a/solution.py
+++ b/solution.py
@@ -9,10 +9,10 @@
 
 MESH = pl.DeviceIdType.MESH
 HALVES = 2
-SLABS = 3
+SLABS = 2
 STREAMS = 4
 CHUNKS_1 = 8
-CHUNKS_2 = 8
+CHUNKS_2 = 6
 BUFFERS = 3
 
 

time: 166 us -> 153 us (0.922)
  Pallas kernels: 164 us -> 151 us
    pallas_call x1, Pallas kernels: 164 us -> 151 us  [on_device(): pl.pallas_call(functools.partial(kernel, R, C), out_shape=jax.ShapeDtypeS...]
where the time goes in v2:
time: 153 us
  Pallas kernels  151 us (99%)
  local copies, waits for them, and re-layouts  2.06 us (1%)
    pallas_call x1, Pallas kernels, on_device(): pl.pallas_call(functools.partial(kernel, R, C), out_shape=jax.ShapeDtypeS...  151 us

profile of v2, /device:TPU:0, one launch (start us, length us, event | category | flops | bytes accessed | tf_op | source)
XLA Modules:
  0.0 153.2 jit_solution(12614405300928216979)
XLA Ops:
  0.0 151.1 %shard_map.28 = bf16[32,12288]{1,0:T(8,128)(2,1)} custom-call(bf16[2048,12288]{1,0:T(8,128)(2,1)} %t2.1, bf16[32,12288]{1,0:T(8,128)(2,1)} %l2.1), custom_call_target="tpu_custom_call" | custom-call | tf_op jit(solution)/shard_map/pallas_call | solution.py:376
  151.1 2.1 %copy.4 = bf16[32,12288]{1,0:T(8,128)(2,1)} copy(bf16[32,12288]{1,0:T(8,128)(2,1)} %shard_map.28) | data formatting | bytes 1572864
